TPU v7x, 32 devices: a whole 2x2x4 slice. The times are simulated.
32 devices in a mesh: dp: 8 (over z, y), fsdp: 4 (over x, core).
Axes of the slice: x: 2, y: 2, z: 4, core: 2. Of those that a mesh axis runs over, the one named last changes fastest.
Arguments:
- hidden_in: bfloat16 [2, 32, 256, 768], P(None, ('dp', 'fsdp')), may hold values from -6 to 6
- patches: bfloat16 [2, 32, 2048, 768], P(None, ('dp', 'fsdp')), may hold values from -6 to 6
- token_segments: int32 [2, 32, 256], P(None, ('dp', 'fsdp')), may hold values from 0 to 3, as said below
- patch_segments: int32 [2, 32, 2048], P(None, ('dp', 'fsdp')), may hold values from 0 to 3, as said below
- cotangent: bfloat16 [2, 32, 256, 768], P(None, ('dp', 'fsdp')), may hold values from -6 to 6
- attention_weights: float32 [8, 768, 768], P(None, 'fsdp', 'dp'), may hold values from -1.1547005 to 1.1547005
- attention_means: float32 [8, 768, 768], P(None, 'fsdp', 'dp'), may hold values from -40 to 40
- attention_squares: float32 [8, 768, 768], P(None, 'fsdp', 'dp'), may hold values from 131.072 to 1638.4
- inner_weights: float32 [2, 768, 2048], P(None, 'fsdp', 'dp'), may hold values from -0.21875 to 0.21875
- inner_means: float32 [2, 768, 2048], P(None, 'fsdp', 'dp'), may hold values from -40 to 40
- inner_squares: float32 [2, 768, 2048], P(None, 'fsdp', 'dp'), may hold values from 131.072 to 1638.4
- outer_weights: float32 [2048, 768], P('fsdp', 'dp'), may hold values from -0.125 to 0.125
- outer_means: float32 [2048, 768], P('fsdp', 'dp'), may hold values from -48 to 48
- outer_squares: float32 [2048, 768], P('fsdp', 'dp'), may hold values from 163.84 to 2457.6
- norm_gains: float32 [3, 768], P(None, 'fsdp'), may hold values from 0.25 to 1.75
- gain_means: float32 [3, 768], P(None, 'fsdp'), may hold values from -80 to 80
- gain_squares: float32 [3, 768], P(None, 'fsdp'), may hold values from 425.984 to 6881.28
Outputs:
- hidden_out: bfloat16 [2, 32, 256, 768], P(None, ('dp', 'fsdp'))
- hidden_grad: float32 [2, 32, 256, 768], P(None, ('dp', 'fsdp'))
- patch_grad: float32 [2, 32, 2048, 768], P(None, ('dp', 'fsdp'))
- attention_mean: float32 [8, 768, 768], P(None, 'fsdp', 'dp')
- attention_square: float32 [8, 768, 768], P(None, 'fsdp', 'dp')
- attention_master: float32 [8, 768, 768], P(None, 'fsdp', 'dp')
- attention_copy: bfloat16 [8, 768, 768], P(None, 'fsdp', 'dp')
- inner_mean: float32 [2, 768, 2048], P(None, 'fsdp', 'dp')
- inner_square: float32 [2, 768, 2048], P(None, 'fsdp', 'dp')
- inner_master: float32 [2, 768, 2048], P(None, 'fsdp', 'dp')
- inner_copy: bfloat16 [2, 768, 2048], P(None, 'fsdp', 'dp')
- outer_mean: float32 [2048, 768], P('fsdp', 'dp')
- outer_square: float32 [2048, 768], P('fsdp', 'dp')
- outer_master: float32 [2048, 768], P('fsdp', 'dp')
- outer_copy: bfloat16 [2048, 768], P('fsdp', 'dp')
- gain_mean: float32 [3, 768], P(None, 'fsdp')
- gain_square: float32 [3, 768], P(None, 'fsdp')
- gain_master: float32 [3, 768], P(None, 'fsdp')
- gain_copy: bfloat16 [3, 768], P(None, 'fsdp')
Inputs may be any that keep to these rules, and one draw needn't show every extreme that they name: `token_segments`: along each row the ids never fall from one token to the next, and each of the 4 ids holds one token or more. `patch_segments`: along each row the ids never fall from one patch to the next, and each of the 4 ids holds one patch or more.
All inputs are finite; a program needn't handle non-finite values.
Results may differ from a plain program's by a relative error of at most 0.02.
The roundings to bfloat16 on the way count: a program that leaves them out, or rounds other values in their place, can miss the bound.
Values may be sent and summed in bfloat16 or wider, within the bound.
A program may use at most 320 MiB of HBM per device.

v0:
```python
import jax
import jax.numpy as jnp
from jax import lax
from jax.sharding import PartitionSpec as P

D = 768
HEADS = 12
HEAD = 64
STEP = 10


epsilon = 1e-06
score_scale = 0.125
masked_value = -1000000000.0
beta_one = 0.9
beta_two = 0.95
adam_epsilon = 1e-08
decay_matrix = 0.1
rate_matrix = 0.1
rate_gain = 0.3
float_type = jnp.float32
brain_type = jnp.bfloat16


def gelu_tanh(values):
    return (
        0.5
        * values
        * (1.0 + jnp.tanh(0.7978845608028654 * (values + 0.044715 * values * values * values)))
    )


def split_heads(matrix):
    return matrix.reshape(matrix.shape[:-1] + (HEADS, HEAD))


def norm_forward(values, gain):
    inverse_rms = lax.rsqrt(jnp.mean(values * values, axis=-1, keepdims=True) + epsilon)
    unit_rows = values * inverse_rms
    return (unit_rows * gain.astype(float_type), unit_rows, inverse_rms)


def norm_backward(grad_rows, gain, unit_rows, inverse_rms):
    grad_unit = grad_rows * gain.astype(float_type)
    grad_values = inverse_rms * (
        grad_unit - unit_rows * jnp.mean(grad_unit * unit_rows, axis=-1, keepdims=True)
    )
    return (grad_values, jnp.sum(grad_rows * unit_rows, axis=0))


def softmax_rows(scores):
    row_maximum = jnp.max(scores, axis=-1, keepdims=True)
    raised = jnp.exp(scores - row_maximum)
    return raised / jnp.sum(raised, axis=-1, keepdims=True)


def attend_forward(queries, key_heads, value_heads, allowed):
    scores = score_scale * jnp.einsum(
        "qhe,khe->hqk", queries, key_heads, preferred_element_type=float_type
    )
    probabilities = softmax_rows(jnp.where(allowed[None], scores, masked_value))
    rounded_probs = probabilities.astype(brain_type)
    mixture = jnp.einsum(
        "hqk,khe->qhe", rounded_probs, value_heads, preferred_element_type=float_type
    )
    return (mixture.astype(brain_type), probabilities, rounded_probs)


def attend_backward(grad_mixture, queries, key_heads, value_heads, probabilities, rounded_probs):
    grad_probs = jnp.einsum(
        "qhe,khe->hqk", grad_mixture, value_heads, preferred_element_type=float_type
    )
    grad_values = jnp.einsum(
        "hqk,qhe->khe", rounded_probs, grad_mixture, preferred_element_type=float_type
    ).astype(brain_type)
    row_inner = jnp.sum(probabilities * grad_probs, axis=-1, keepdims=True)
    grad_scores = (probabilities * (grad_probs - row_inner)).astype(brain_type)
    grad_queries = (
        score_scale
        * jnp.einsum("hqk,khe->qhe", grad_scores, key_heads, preferred_element_type=float_type)
    ).astype(brain_type)
    grad_keys = (
        score_scale
        * jnp.einsum("hqk,qhe->khe", grad_scores, queries, preferred_element_type=float_type)
    ).astype(brain_type)
    return (grad_queries, grad_keys, grad_values)


def layer_forward(weights, hidden, patch_rows, token_ids, patch_ids):
    attention, inner_matrix, outer_matrix, gain_rows = weights
    length = hidden.shape[0]
    initial = hidden.astype(float_type)
    normed_one, unit_one, rms_one = norm_forward(initial, gain_rows[0])
    normed_one = normed_one.astype(brain_type)
    projected = jnp.einsum(
        "nd,kde->kne", normed_one, attention[0:3], preferred_element_type=float_type
    ).astype(brain_type)
    heads_in = split_heads(projected)
    places = jnp.arange(length)
    causal = (places[:, None] >= places[None, :]) & (token_ids[:, None] == token_ids[None, :])
    mixture_one, probs_one, rounded_one = attend_forward(
        heads_in[0], heads_in[1], heads_in[2], causal
    )
    mixture_one = mixture_one.reshape(length, D)
    after_one = initial + jnp.dot(mixture_one, attention[3], preferred_element_type=float_type)
    normed_two, unit_two, rms_two = norm_forward(after_one, gain_rows[1])
    normed_two = normed_two.astype(brain_type)
    cross_query = split_heads(
        jnp.dot(normed_two, attention[4], preferred_element_type=float_type).astype(brain_type)
    )
    cross_pair = split_heads(
        jnp.einsum(
            "pd,kde->kpe", patch_rows, attention[5:7], preferred_element_type=float_type
        ).astype(brain_type)
    )
    matching = token_ids[:, None] == patch_ids[None, :]
    mixture_two, probs_two, rounded_two = attend_forward(
        cross_query, cross_pair[0], cross_pair[1], matching
    )
    mixture_two = mixture_two.reshape(length, D)
    after_two = after_one + jnp.dot(mixture_two, attention[7], preferred_element_type=float_type)
    normed_three, unit_three, rms_three = norm_forward(after_two, gain_rows[2])
    normed_three = normed_three.astype(brain_type)
    gated = jnp.einsum("nd,kdf->knf", normed_three, inner_matrix, preferred_element_type=float_type)
    units = (gelu_tanh(gated[0]) * gated[1]).astype(brain_type)
    layer_out = (
        after_two + jnp.dot(units, outer_matrix, preferred_element_type=float_type)
    ).astype(brain_type)
    stored = {
        "unit_one": unit_one,
        "rms_one": rms_one,
        "normed_one": normed_one,
        "heads_in": heads_in,
        "probs_one": probs_one,
        "rounded_one": rounded_one,
        "mixture_one": mixture_one,
        "unit_two": unit_two,
        "rms_two": rms_two,
        "normed_two": normed_two,
        "cross_query": cross_query,
        "cross_pair": cross_pair,
        "probs_two": probs_two,
        "rounded_two": rounded_two,
        "mixture_two": mixture_two,
        "unit_three": unit_three,
        "rms_three": rms_three,
        "normed_three": normed_three,
        "gated": gated,
        "units": units,
    }
    return (layer_out, stored)


def layer_backward(weights, stored, cotangent_row, patch_rows):
    attention, inner_matrix, outer_matrix, gain_rows = weights
    length = cotangent_row.shape[0]
    grad_final = cotangent_row.astype(float_type)
    grad_low = grad_final.astype(brain_type)
    grad_outer = jnp.einsum(
        "nf,nd->fd", stored["units"], grad_low, preferred_element_type=float_type
    )
    grad_units = jnp.einsum("nd,fd->nf", grad_low, outer_matrix, preferred_element_type=float_type)
    gate_in = stored["gated"][0]
    up_in = stored["gated"][1]
    activation, gelu_back = jax.vjp(gelu_tanh, gate_in)
    grad_gate = gelu_back(grad_units * up_in)[0]
    grad_gated = jnp.stack([grad_gate, grad_units * activation]).astype(brain_type)
    grad_inner = jnp.einsum(
        "nd,knf->kdf", stored["normed_three"], grad_gated, preferred_element_type=float_type
    )
    grad_normed = jnp.einsum(
        "knf,kdf->nd", grad_gated, inner_matrix, preferred_element_type=float_type
    )
    grad_from_three, gain_three = norm_backward(
        grad_normed, gain_rows[2], stored["unit_three"], stored["rms_three"]
    )
    grad_after_two = grad_final + grad_from_three
    branch_two = grad_after_two.astype(brain_type)
    grad_cross_out = jnp.einsum(
        "nd,ne->de", stored["mixture_two"], branch_two, preferred_element_type=float_type
    )
    grad_mixture_two = split_heads(
        jnp.einsum("ne,de->nd", branch_two, attention[7], preferred_element_type=float_type).astype(
            brain_type
        )
    )
    cross_pair = stored["cross_pair"]
    grad_cq, grad_ck, grad_cv = attend_backward(
        grad_mixture_two,
        stored["cross_query"],
        cross_pair[0],
        cross_pair[1],
        stored["probs_two"],
        stored["rounded_two"],
    )
    grad_cq = grad_cq.reshape(length, D)
    grad_pair = jnp.stack([grad_ck, grad_cv]).reshape(2, patch_rows.shape[0], D)
    grad_cross_query = jnp.einsum(
        "nd,ne->de", stored["normed_two"], grad_cq, preferred_element_type=float_type
    )
    grad_cross_pair = jnp.einsum(
        "pd,kpe->kde", patch_rows, grad_pair, preferred_element_type=float_type
    )
    patch_grad = jnp.einsum(
        "kpe,kde->pd", grad_pair, attention[5:7], preferred_element_type=float_type
    )
    grad_normed_two = jnp.einsum(
        "ne,de->nd", grad_cq, attention[4], preferred_element_type=float_type
    )
    grad_from_two, gain_two = norm_backward(
        grad_normed_two, gain_rows[1], stored["unit_two"], stored["rms_two"]
    )
    grad_after_one = grad_after_two + grad_from_two
    branch_one = grad_after_one.astype(brain_type)
    grad_self_out = jnp.einsum(
        "nd,ne->de", stored["mixture_one"], branch_one, preferred_element_type=float_type
    )
    grad_mixture_one = split_heads(
        jnp.einsum("ne,de->nd", branch_one, attention[3], preferred_element_type=float_type).astype(
            brain_type
        )
    )
    heads_in = stored["heads_in"]
    grad_query, grad_key, grad_value = attend_backward(
        grad_mixture_one,
        heads_in[0],
        heads_in[1],
        heads_in[2],
        stored["probs_one"],
        stored["rounded_one"],
    )
    grad_projected = jnp.stack([grad_query, grad_key, grad_value]).reshape(3, length, D)
    grad_self_in = jnp.einsum(
        "nd,kne->kde", stored["normed_one"], grad_projected, preferred_element_type=float_type
    )
    grad_normed_one = jnp.einsum(
        "kne,kde->nd", grad_projected, attention[0:3], preferred_element_type=float_type
    )
    grad_from_one, gain_one = norm_backward(
        grad_normed_one, gain_rows[0], stored["unit_one"], stored["rms_one"]
    )
    hidden_grad = grad_after_one + grad_from_one
    grad_attention = jnp.concatenate(
        [
            grad_self_in,
            grad_self_out[None],
            grad_cross_query[None],
            grad_cross_pair,
            grad_cross_out[None],
        ],
        axis=0,
    )
    grad_gains = jnp.stack([gain_one, gain_two, gain_three])
    return (hidden_grad, patch_grad, (grad_attention, grad_inner, grad_outer, grad_gains))


def fetch_forward(copies):
    widened = (
        lax.all_gather(copies[0], "fsdp", axis=1, tiled=True),
        lax.all_gather(copies[1], "fsdp", axis=1, tiled=True),
        lax.all_gather(copies[2], "fsdp", axis=0, tiled=True),
        lax.all_gather(copies[3], "fsdp", axis=1, tiled=True),
    )
    complete = (
        lax.all_gather(widened[0], "dp", axis=2, tiled=True),
        lax.all_gather(widened[1], "dp", axis=2, tiled=True),
        lax.all_gather(widened[2], "dp", axis=1, tiled=True),
    )
    return (complete[0], complete[1], complete[2], widened[3])


def fetch_backward(copies):
    widened = (
        lax.all_gather(copies[0], "fsdp", axis=1, tiled=True),
        lax.all_gather(copies[1], "fsdp", axis=1, tiled=True),
        lax.all_gather(copies[2], "fsdp", axis=0, tiled=True),
        lax.all_gather(copies[3], "fsdp", axis=1, tiled=True),
    )
    complete = (
        lax.all_gather(widened[0], "dp", axis=2, tiled=True),
        lax.all_gather(widened[1], "dp", axis=2, tiled=True),
        lax.all_gather(widened[2], "dp", axis=1, tiled=True),
    )
    return (complete[0], complete[1], complete[2], widened[3])


def reduce_grads(totals):
    partial_sums = (
        lax.psum_scatter(totals[0], "dp", scatter_dimension=2, tiled=True),
        lax.psum_scatter(totals[1], "dp", scatter_dimension=2, tiled=True),
        lax.psum_scatter(totals[2], "dp", scatter_dimension=1, tiled=True),
    )
    gain_totals = lax.psum(totals[3], "dp")
    return (
        lax.psum_scatter(partial_sums[0], "fsdp", scatter_dimension=1, tiled=True),
        lax.psum_scatter(partial_sums[1], "fsdp", scatter_dimension=1, tiled=True),
        lax.psum_scatter(partial_sums[2], "fsdp", scatter_dimension=0, tiled=True),
        lax.psum_scatter(gain_totals, "fsdp", scatter_dimension=1, tiled=True),
    )


def adam_update(weight, mean_old, square_old, gradient, step_rate, decay_rate):
    mean_new = beta_one * mean_old + (1.0 - beta_one) * gradient
    square_new = beta_two * square_old + (1.0 - beta_two) * gradient * gradient
    corrected = (
        mean_new
        / (1.0 - beta_one**STEP)
        / (jnp.sqrt(square_new / (1.0 - beta_two**STEP)) + adam_epsilon)
    )
    master = weight - step_rate * (corrected + decay_rate * weight)
    return (mean_new, square_new, master, master.astype(jnp.bfloat16))


def on_device(
    hidden_in,
    patches,
    token_segments,
    patch_segments,
    cotangent,
    attention_weights,
    attention_means,
    attention_squares,
    inner_weights,
    inner_means,
    inner_squares,
    outer_weights,
    outer_means,
    outer_squares,
    norm_gains,
    gain_means,
    gain_squares,
):
    copies = (
        attention_weights.astype(brain_type),
        inner_weights.astype(brain_type),
        outer_weights.astype(brain_type),
        norm_gains.astype(brain_type),
    )
    layer_outputs = []
    input_grads = []
    patch_grads = []
    totals = None
    for batch_index in range(hidden_in.shape[0]):
        forward_weights = fetch_forward(copies)
        layer_out, stored = layer_forward(
            forward_weights,
            hidden_in[batch_index, 0],
            patches[batch_index, 0],
            token_segments[batch_index, 0],
            patch_segments[batch_index, 0],
        )
        backward_weights = fetch_backward(copies)
        hidden_grad, patch_grad, gradients = layer_backward(
            backward_weights, stored, cotangent[batch_index, 0], patches[batch_index, 0]
        )
        layer_outputs.append(layer_out)
        input_grads.append(hidden_grad)
        patch_grads.append(patch_grad)
        totals = gradients if totals is None else jax.tree.map(jnp.add, totals, gradients)
    owned_grads = reduce_grads(totals)
    attention_new = adam_update(
        attention_weights,
        attention_means,
        attention_squares,
        owned_grads[0],
        rate_matrix,
        decay_matrix,
    )
    inner_new = adam_update(
        inner_weights, inner_means, inner_squares, owned_grads[1], rate_matrix, decay_matrix
    )
    outer_new = adam_update(
        outer_weights, outer_means, outer_squares, owned_grads[2], rate_matrix, decay_matrix
    )
    gain_new = adam_update(norm_gains, gain_means, gain_squares, owned_grads[3], rate_gain, 0.0)
    hidden_out = jnp.stack(layer_outputs)[:, None]
    hidden_grads = jnp.stack(input_grads)[:, None]
    patch_grads_all = jnp.stack(patch_grads)[:, None]
    return (
        hidden_out,
        hidden_grads,
        patch_grads_all,
        attention_new[0],
        attention_new[1],
        attention_new[2],
        attention_new[3],
        inner_new[0],
        inner_new[1],
        inner_new[2],
        inner_new[3],
        outer_new[0],
        outer_new[1],
        outer_new[2],
        outer_new[3],
        gain_new[0],
        gain_new[1],
        gain_new[2],
        gain_new[3],
    )


def solution(mesh):
    placed = (
        P(None, ("dp", "fsdp"), None, None),
        P(None, ("dp", "fsdp"), None, None),
        P(None, ("dp", "fsdp"), None),
        P(None, ("dp", "fsdp"), None),
        P(None, ("dp", "fsdp"), None, None),
        P(None, "fsdp", "dp"),
        P(None, "fsdp", "dp"),
        P(None, "fsdp", "dp"),
        P(None, "fsdp", "dp"),
        P(None, "fsdp", "dp"),
        P(None, "fsdp", "dp"),
        P("fsdp", "dp"),
        P("fsdp", "dp"),
        P("fsdp", "dp"),
        P(None, "fsdp"),
        P(None, "fsdp"),
        P(None, "fsdp"),
    )
    return jax.shard_map(
        on_device,
        mesh=mesh,
        in_specs=placed,
        out_specs=(
            P(None, ("dp", "fsdp"), None, None),
            P(None, ("dp", "fsdp"), None, None),
            P(None, ("dp", "fsdp"), None, None),
            P(None, "fsdp", "dp"),
            P(None, "fsdp", "dp"),
            P(None, "fsdp", "dp"),
            P(None, "fsdp", "dp"),
            P(None, "fsdp", "dp"),
            P(None, "fsdp", "dp"),
            P(None, "fsdp", "dp"),
            P(None, "fsdp", "dp"),
            P("fsdp", "dp"),
            P("fsdp", "dp"),
            P("fsdp", "dp"),
            P("fsdp", "dp"),
            P(None, "fsdp"),
            P(None, "fsdp"),
            P(None, "fsdp"),
            P(None, "fsdp"),
        ),
        check_vma=False,
    )
```

profile of v0, /device:TPU:0, one launch (start us, length us, event | category | flops | bytes accessed | tf_op | source)
XLA Modules:
  0.0 1277.1 jit_solution(9727439426056397318)
XLA Ops:
  9.8 22.8 %all-gather.6.cloned.1.call-done = bf16[8,768,96]{2,0,1:T(8,128)(2,1)} async-done(((bf16[8,192,96]{2,0,1:T(8,128)(2,1)}), bf16[8,768,96]{2,0,1:T(8,128)(2,1)}) %all-gather.6.cloned.1.call-update) | async-done | bytes 1179664 | tf_op jit(solution)/shard_map/all_gather | solution.py:259
  35.8 9.0 all_gather.17
  45.2 5.2 all-gather
  54.9 118.2 %all-gather.8.cloned.1.call-done = bf16[8,768,768]{1,0,2:T(8,128)(2,1)} async-done(((bf16[8,768,96]{1,0,2:T(8,128)(2,1)}), bf16[8,768,768]{1,0,2:T(8,128)(2,1)}) %all-gather.8.cloned.1.call-update) | async-done | bytes 9437200 | tf_op jit(solution)/shard_map/all_gather | solution.py:265
  173.2 7.1 slice.179
  180.2 8.3 copy.479
  188.5 18.3 %fusion.261 = (bf16[1,768,768]{1,0,2:T(2,128)(2,1)}, bf16[1,768,768]{1,0,2:T(2,128)(2,1)}, bf16[1,768,768]{1,0,2:T(2,128)(2,1)}) fusion(bf16[8,768,768]{1,0,2:T(8,128)(2,1)} %all-gather.8.cloned.1.call-done), kind=kLoop, calls=%fused_computation.380 | loop fusion | bytes 7077888 | tf_op jit(solution)/shard_map/slice | solution.py:121
  206.8 5.4 copy.480
  212.2 5.7 copy.482
  249.8 6.7 slice.184
  256.6 5.8 convert_bitcast_fusion.1
  265.6 14.4 %fusion.271 = (f32[12,256]{1,0:T(8,128)S(1)}, f32[12,256,2048]{2,1,0:T(8,128)}) fusion(pred[256,2048]{1,0:T(8,128)(4,1)} %broadcast_compare_fusion.1, bf16[256,12,64]{0,2,1:T(8,128)(2,1)S(1)} %bitcast.442, bf16[2048,12,64]{0,2,1:T(8,128)(2,1)} %bitcast.427), kind=kOutput, calls=%fused_computation.390 | convolution fusion | flops 830474240 | bytes 29241344 | tf_op jit(solution)/shard_map/sub | solution.py:53
  280.6 5.4 copy.483
  287.0 11.6 fusion.101
  300.7 7.4 convert_bitcast_fusion
  311.3 14.4 %fusion.269 = (f32[12,256]{1,0:T(8,128)S(1)}, f32[12,256,2048]{2,1,0:T(8,128)}) fusion(pred[256,2048]{1,0:T(8,128)(4,1)} %broadcast_compare_fusion, bf16[256,12,64]{0,2,1:T(8,128)(2,1)S(1)} %bitcast.444, bf16[2048,12,64]{0,2,1:T(8,128)(2,1)} %bitcast.429), kind=kOutput, calls=%fused_computation.388 | convolution fusion | flops 830474240 | bytes 29241344 | tf_op jit(solution)/shard_map/sub | solution.py:53
  325.8 11.5 fusion.104
  338.1 4.9 convolution_bitcast_fusion.1
  355.5 116.4 %reduce-scatter.15.cloned.1.call-done = f32[2048,96]{0,1:T(8,128)} async-done(((f32[2048,768]{0,1:T(8,128)}), f32[2048,96]{0,1:T(8,128)}) %reduce-scatter.15.cloned.1.call-update) | async-done | bytes 786448 | tf_op jit(solution)/shard_map/reduce_scatter | solution.py:291
  471.9 24.8 %reduce-scatter.17.cloned.1.call-done = f32[512,96]{0,1:T(8,128)} async-done(((f32[2048,96]{0,1:T(8,128)}), f32[512,96]{0,1:T(8,128)}) %reduce-scatter.17.cloned.1.call-update) | async-done | bytes 196624 | tf_op jit(solution)/shard_map/reduce_scatter | solution.py:297
  498.9 6.6 all_gather.19
  505.6 60.4 %all-gather.12.cloned.1.call-done = bf16[2048,768]{0,1:T(8,128)(2,1)} async-done(((bf16[2048,96]{0,1:T(8,128)(2,1)}), bf16[2048,768]{0,1:T(8,128)(2,1)}) %all-gather.12.cloned.1.call-update) | async-done | bytes 3145744 | tf_op jit(solution)/shard_map/all_gather | solution.py:267
  566.0 5.9 fusion.147
  571.9 7.8 fusion.89
  591.4 11.2 fusion.29
  602.6 18.0 %multiply_reduce_fusion = (f32[12,256]{1,0:T(8,128)}, f32[12,256,2048]{2,1,0:T(8,128)}) fusion(f32[12,256,2048]{2,1,0:T(8,128)} %get-tuple-element.202, f32[12,256]{1,0:T(8,128)} %copy-done.110, bf16[256,12,64]{0,2,1:T(8,128)(2,1)} %bitcast.478, bf16[2048,12,64]{0,2,1:T(8,128)(2,1)} %bitcast.441), kind=kOutput, calls=%fused_computation.5 | convolution fusion | flops 824177664 | bytes 53895168 | tf_op jit(solution)/shard_map/qhe,khe->hqk/dot_general | solution.py:70
  621.4 11.8 add_bitcast_fusion
  633.9 12.0 fusion.26
  645.9 4.8 copy.421
  653.6 16.7 %multiply_convert_fusion = bf16[12,256,2048]{2,1,0:T(8,128)(2,1)S(1)} fusion(f32[12,256,2048]{2,1,0:T(8,128)} %get-tuple-element.215, f32[12,256]{1,0:T(8,128)} %get-tuple-element.214, f32[12,256,2048]{2,1,0:T(8,128)} %get-tuple-element.202, f32[12,256]{1,0:T(8,128)} %copy-done.110), kind=kLoop, calls=%fused_computation.4 | loop fusion | flops 25165824 | bytes 62939136 | tf_op jit(solution)/shard_map/convert_element_type | solution.py:77
  677.7 17.6 %multiply_reduce_fusion.1 = (f32[12,256]{1,0:T(8,128)S(1)}, f32[12,256,2048]{2,1,0:T(8,128)}) fusion(f32[12,256,2048]{2,1,0:T(8,128)} %get-tuple-element.208, f32[12,256]{1,0:T(8,128)S(1)} %copy-done.109, bf16[256,12,64]{0,2,1:T(8,128)(2,1)S(1)} %bitcast.472, bf16[2048,12,64]{0,2,1:T(8,128)(2,1)} %bitcast.439), kind=kOutput, calls=%fused_computation.7 | convolution fusion | flops 824177664 | bytes 53895168 | tf_op jit(solution)/shard_map/qhe,khe->hqk/dot_general | solution.py:70
  695.3 16.5 %multiply_convert_fusion.1 = bf16[12,256,2048]{2,1,0:T(8,128)(2,1)S(1)} fusion(f32[12,256,2048]{2,1,0:T(8,128)} %get-tuple-element.217, f32[12,256]{1,0:T(8,128)S(1)} %get-tuple-element.216, f32[12,256,2048]{2,1,0:T(8,128)} %get-tuple-element.208, f32[12,256]{1,0:T(8,128)S(1)} %copy-done.109), kind=kLoop, calls=%fused_computation.6 | loop fusion | flops 25165824 | bytes 62939136 | tf_op jit(solution)/shard_map/convert_element_type | solution.py:77
  719.9 9.8 fusion.99
  731.7 8.8 fusion.100
  784.2 7.4 bitcast_dynamic-update-slice_fusion.2
  801.4 8.9 bitcast_dynamic-update-slice_fusion.3
  812.3 13.1 %add.227 = f32[8,768,768]{1,2,0:T(8,128)} add(f32[8,768,768]{1,2,0:T(8,128)} %bitcast_dynamic-update-slice_fusion.7, f32[8,768,768]{1,2,0:T(8,128)S(1)} %bitcast_dynamic-update-slice_fusion.4) | non-fusion elementwise | flops 4718592 | bytes 56623104 | tf_op jit(solution)/shard_map/add | solution.py:359
  833.7 5.7 reduce-scatter.13.cloned.1.call-done
  850.4 4.6 fusion.107
  855.0 299.2 %reduce-scatter.11.cloned.1.call-done = f32[8,768,96]{1,2,0:T(8,128)} async-done(((f32[8,768,768]{1,2,0:T(8,128)}), f32[8,768,96]{1,2,0:T(8,128)}) %reduce-scatter.11.cloned.1.call-update) | async-done | bytes 2359312 | tf_op jit(solution)/shard_map/reduce_scatter | solution.py:289
  1157.8 4.5 reshape.396
  1162.4 4.9 fusion.108
  1172.5 5.2 fusion.25
  1177.7 6.9 fusion.24
  1184.6 9.1 maximum_bitcast_fusion
  1194.7 19.9 %psum.8 = f32[3,192]{1,0:T(4,128)S(1)} all-reduce(f32[3,192]{1,0:T(4,128)S(1)} %copy.478), channel_id=1, replica_groups=mesh['dp'=8,'fsdp'=4] {'dp'}, use_global_device_ids=true, to_apply=%region_36.37 | all-reduce | flops 576 | bytes 4608 | tf_op jit(solution)/shard_map/psum | solution.py:293
  1215.2 7.1 all-reduce.3.cloned.1.call-done
  1226.0 31.7 %reduce-scatter.19.cloned.1.call-done = f32[192,768]{1,0:T(8,128)} async-done(((f32[768,768]{1,0:T(8,128)}), f32[192,768]{1,0:T(8,128)}) %reduce-scatter.19.cloned.1.call-update) | async-done | bytes 589840
  (425 shorter events, 200.9 us)
Async XLA Ops:
  7.2 28.6 %copy-start.75 = (f32[2,192,256]{2,1,0:T(8,128)S(1)}, f32[2,192,256]{2,1,0:T(8,128)}, u32[]{:S(2)}) copy-start(f32[2,192,256]{2,1,0:T(8,128)} %param.25) | copy-start | bytes 1179652
  7.2 25.3 %all-gather.6.cloned.1.call-start = ((), (), s32[]{:S(2)}) async-start(), calls=%async_computation.6 | async-start | bytes 1966080 | tf_op jit(solution)/shard_map/all_gather | solution.py:259
  9.7 35.3 %copy-start.111 = (f32[3,192]{1,0:T(4,128)S(1)}, f32[3,192]{1,0:T(4,128)}, u32[]{:S(2)}) copy-start(f32[3,192]{1,0:T(4,128)} %param.31) | copy-start | bytes 6916
  9.7 35.3 %copy-start.127 = (s32[2,1,256]{2,1,0:T(1,128)S(1)}, s32[2,1,256]{2,1,0:T(1,128)}, u32[]{:S(2)}) copy-start(s32[2,1,256]{2,1,0:T(1,128)} %param.19) | copy-start | bytes 6148
  9.7 35.3 %copy-start.47 = (bf16[2,1,256,768]{3,2,1,0:T(8,128)(2,1)S(1)}, bf16[2,1,256,768]{3,2,1,0:T(8,128)(2,1)}, u32[]{:S(2)}) copy-start(bf16[2,1,256,768]{3,2,1,0:T(8,128)(2,1)} %param.17) | copy-start | bytes 2359300
  9.7 41.4 %copy-start.113 = (s32[2,1,2048]{2,1,0:T(1,128)S(1)}, s32[2,1,2048]{2,1,0:T(1,128)}, u32[]{:S(2)}) copy-start(s32[2,1,2048]{2,1,0:T(1,128)} %param.20) | copy-start | bytes 49156
  9.7 163.5 %all-gather.8.cloned.1.call-start = ((), (), s32[]{:S(2)}) async-start(), calls=%async_computation.7 | async-start | bytes 10616832 | tf_op jit(solution)/shard_map/all_gather | solution.py:265
  35.8 302.3 %all-gather.10.cloned.1.call-start = ((), (), s32[]{:S(2)}) async-start(), calls=%async_computation.8 | async-start | bytes 7077888 | tf_op jit(solution)/shard_map/all_gather | solution.py:266
  44.9 427.0 %reduce-scatter.15.cloned.1.call-start = ((), (), s32[]{:S(2)}) async-start(), calls=%async_computation.12 | async-start | bytes 7077888 | tf_op jit(solution)/shard_map/reduce_scatter | solution.py:291
  51.1 175.6 %copy-start.115 = (f32[768]{0:T(1024)}, f32[768]{0:T(1024)S(1)}, u32[]{:S(2)}) copy-start(f32[768]{0:T(1024)S(1)} %get-tuple-element.151) | copy-start | bytes 9220
  51.1 228.9 %copy-start.99 = (f32[768]{0:T(1024)}, f32[768]{0:T(1024)S(1)}, u32[]{:S(2)}) copy-start(f32[768]{0:T(1024)S(1)} %get-tuple-element.150) | copy-start | bytes 9220
  54.9 163.0 %copy-start.121 = (f32[256]{0:T(256)}, f32[256]{0:T(256)S(1)}, u32[]{:S(2)}) copy-start(f32[256]{0:T(256)S(1)} %get-tuple-element.225) | copy-start | bytes 3076
  54.9 171.8 %copy-start.123 = (f32[256]{0:T(256)}, f32[256]{0:T(256)S(1)}, u32[]{:S(2)}) copy-start(f32[256]{0:T(256)S(1)} %get-tuple-element.226) | copy-start | bytes 3076
  212.2 28.9 %copy-start.27 = (bf16[1,768,768]{2,1,0:T(8,128)(2,1)}, bf16[1,768,768]{2,1,0:T(8,128)(2,1)S(1)}, u32[]{:S(2)}) copy-start(bf16[1,768,768]{2,1,0:T(8,128)(2,1)S(1)} %copy.480) | copy-start | bytes 3538948
  217.9 62.2 %copy-start.4 = (bf16[1,768,768]{2,1,0:T(8,128)(2,1)}, bf16[1,768,768]{2,1,0:T(8,128)(2,1)S(1)}, u32[]{:S(2)}) copy-start(bf16[1,768,768]{2,1,0:T(8,128)(2,1)S(1)} %copy.482) | copy-start | bytes 3538948
  224.7 17.9 %copy-start.64 = (bf16[1,256,768]{1,2,0:T(8,128)(2,1)}, bf16[1,256,768]{1,2,0:T(8,128)(2,1)S(1)}, u32[]{:S(2)}) copy-start(bf16[1,256,768]{1,2,0:T(8,128)(2,1)S(1)} %copy.400) | copy-start | bytes 1179652
  241.7 56.9 %copy-start.8 = (f32[256,768]{1,0:T(8,128)}, f32[256,768]{1,0:T(8,128)S(1)}, u32[]{:S(2)}) copy-start(f32[256,768]{1,0:T(8,128)S(1)} %get-tuple-element.206) | copy-start | bytes 2359300
  242.6 23.1 %copy-start.60 = (bf16[256,768]{0,1:T(8,128)(2,1)}, bf16[256,768]{0,1:T(8,128)(2,1)S(1)}, u32[]{:S(2)}) copy-start(bf16[256,768]{0,1:T(8,128)(2,1)S(1)} %copy.397) | copy-start | bytes 1179652
  246.6 10.0 slice-start.2
  246.6 9.9 slice-start.3
  249.7 87.6 %copy-start.10 = (f32[256,768]{1,0:T(8,128)}, f32[256,768]{1,0:T(8,128)S(1)}, u32[]{:S(2)}) copy-start(f32[256,768]{1,0:T(8,128)S(1)} %get-tuple-element.200) | copy-start | bytes 2359300
  249.8 30.2 %copy-start.103 = (f32[256]{0:T(256)}, f32[256]{0:T(256)S(1)}, u32[]{:S(2)}) copy-start(f32[256]{0:T(256)S(1)} %add_rsqrt_fusion.1) | copy-start | bytes 3076
  299.2 289.5 %copy-start.12 = (f32[256,768]{1,0:T(8,128)}, f32[256,768]{1,0:T(8,128)S(1)}, u32[]{:S(2)}) copy-start(f32[256,768]{1,0:T(8,128)S(1)} %get-tuple-element.210) | copy-start | bytes 2359300
  325.8 11.5 copy-start.110
  338.1 283.3 %copy-start.14 = (f32[256,768]{1,0:T(8,128)}, f32[256,768]{1,0:T(8,128)S(1)}, u32[]{:S(2)}) copy-start(f32[256,768]{1,0:T(8,128)S(1)} %get-tuple-element.212) | copy-start | bytes 2359300
  355.5 141.3 %reduce-scatter.17.cloned.1.call-start = ((), (), s32[]{:S(2)}) async-start(), calls=%async_computation.13 | async-start | bytes 983040 | tf_op jit(solution)/shard_map/reduce_scatter | solution.py:297
  471.9 94.1 %all-gather.12.cloned.1.call-start = ((), (), s32[]{:S(2)}) async-start(), calls=%async_computation.9 | async-start | bytes 3538944 | tf_op jit(solution)/shard_map/all_gather | solution.py:267
  505.5 333.9 %reduce-scatter.13.cloned.1.call-start = ((), (), s32[]{:S(2)}) async-start(), calls=%async_computation.11 | async-start | bytes 14155776 | tf_op jit(solution)/shard_map/reduce_scatter | solution.py:290
  571.9 12.2 slice-start
  590.0 12.7 copy-start.18
  602.6 18.0 %copy-start.23 = (f32[256,768]{1,0:T(8,128)S(1)}, f32[256,768]{1,0:T(8,128)}, u32[]{:S(2)}) copy-start(f32[256,768]{1,0:T(8,128)} %get-tuple-element.187) | copy-start | bytes 2359300
  633.2 521.0 %reduce-scatter.11.cloned.1.call-start = ((), (), s32[]{:S(2)}) async-start(), calls=%async_computation.10 | async-start | bytes 21233664 | tf_op jit(solution)/shard_map/reduce_scatter | solution.py:289
  653.6 16.7 %copy-start.63 = (bf16[256,768]{0,1:T(8,128)(2,1)S(1)}, bf16[256,768]{0,1:T(8,128)(2,1)}, u32[]{:S(2)}) copy-start(bf16[256,768]{0,1:T(8,128)(2,1)} %copy.403) | copy-start | bytes 1179652
  695.3 16.6 %copy-start.61 = (bf16[256,768]{0,1:T(8,128)(2,1)S(1)}, bf16[256,768]{0,1:T(8,128)(2,1)}, u32[]{:S(2)}) copy-start(bf16[256,768]{0,1:T(8,128)(2,1)} %copy-done.60) | copy-start | bytes 1179652
  719.9 9.8 copy-start.5
  719.9 9.8 copy-start.9
  729.7 10.9 copy-start.31
  825.4 368.3 %reduce-scatter.21.cloned.1.call-start = ((), (), s32[]{:S(2)}) async-start(), calls=%async_computation.15 | async-start | bytes 491520
  832.6 10.5 copy-start.44
  833.6 388.7 %all-reduce.3.cloned.1.call-start = ((), (), s32[]{:S(2)}) async-start(), calls=%async_computation.16 | async-start | bytes 3145728
  843.1 414.7 %reduce-scatter.19.cloned.1.call-start = ((), (), s32[]{:S(2)}) async-start(), calls=%async_computation.14 | async-start | bytes 2949120
  1184.6 30.0 %copy-start.112 = (f32[3,192]{1,0:T(4,128)S(1)}, f32[3,192]{1,0:T(4,128)}, u32[]{:S(2)}) copy-start(f32[3,192]{1,0:T(4,128)} %param.31) | copy-start | bytes 6916
  1184.6 30.0 %copy-start.117 = (f32[3,192]{1,0:T(4,128)S(1)}, f32[3,192]{1,0:T(4,128)}, u32[]{:S(2)}) copy-start(f32[3,192]{1,0:T(4,128)} %param.33) | copy-start | bytes 6916
  1184.6 30.0 %copy-start.118 = (f32[3,192]{1,0:T(4,128)S(1)}, f32[3,192]{1,0:T(4,128)}, u32[]{:S(2)}) copy-start(f32[3,192]{1,0:T(4,128)} %param.32) | copy-start | bytes 6916
  1184.6 38.9 %copy-start.76 = (f32[2,192,256]{2,1,0:T(8,128)S(1)}, f32[2,192,256]{2,1,0:T(8,128)}, u32[]{:S(2)}) copy-start(f32[2,192,256]{2,1,0:T(8,128)} %param.25) | copy-start | bytes 1179652
  1223.5 37.0 %copy-start.52 = (f32[8,192,96]{1,2,0:T(8,128)S(1)}, f32[8,192,96]{1,2,0:T(8,128)}, u32[]{:S(2)}) copy-start(f32[8,192,96]{1,2,0:T(8,128)} %copy.439) | copy-start | bytes 1769476
  1223.5 37.0 %copy-start.53 = (f32[8,192,96]{1,2,0:T(8,128)S(1)}, f32[8,192,96]{1,2,0:T(8,128)}, u32[]{:S(2)}) copy-start(f32[8,192,96]{1,2,0:T(8,128)} %copy.426) | copy-start | bytes 1769476
  1223.5 37.0 %copy-start.54 = (f32[8,192,96]{1,2,0:T(8,128)S(1)}, f32[8,192,96]{1,2,0:T(8,128)}, u32[]{:S(2)}) copy-start(f32[8,192,96]{1,2,0:T(8,128)} %copy.437) | copy-start | bytes 1769476
  (99 other events, 379.9 us)
Sparse Core Ops, SparseCore 0:
  10.1 22.3 all-gather.5
  35.9 137.2 all-gather.7
  175.2 97.6 all-gather.9
  355.6 116.2 reduce-scatter.14
  474.2 22.4 reduce-scatter.16
  505.7 60.2 all-gather.11
  633.3 206.0 reduce-scatter.12
  843.3 310.8 reduce-scatter.10
  1157.3 19.8 reduce-scatter.20
  1179.4 42.8 all-reduce.2
  1224.9 32.8 reduce-scatter.18
where the time goes:
time: 1280 us
  waiting for transfers between devices  686 us (54%)
  matrix products  296 us (23%)
  local copies, waits for them, and re-layouts  161 us (13%)
  other arithmetic  75.5 us (6%)
  blocking collectives  40.7 us (3%)
  between operations  16.7 us (1%)
    reduce_scatter x1, waiting for transfers between devices, reduce_grads(): lax.psum_scatter(totals[0], 'dp', scatter_dimension=2, tiled=True)  299 us
    all_gather x1, waiting for transfers between devices, fetch_forward(): lax.all_gather(widened[0], 'dp', axis=2, tiled=True)  118 us
    reduce_scatter x1, waiting for transfers between devices, reduce_grads(): lax.psum_scatter(totals[2], 'dp', scatter_dimension=1, tiled=True)  116 us
    unnamed x293, local copies, waits for them, and re-layouts  80.4 us
    all_gather x1, waiting for transfers between devices, fetch_forward(): lax.all_gather(widened[2], 'dp', axis=1, tiled=True)  60.4 us
    dot_general x4, matrix products, attend_backward(): jnp.einsum('qhe,khe->hqk', grad_mixture, value_heads, preferred_element_t...  41.4 us
    unnamed x14, waiting for transfers between devices  39 us
    sub x4, matrix products, softmax_rows(): raised = jnp.exp(scores - row_maximum)  37.1 us
  transfers between devices with their start and end apart: 11, of which 9 were waited for; matrix products, arithmetic and copies ran while one was open for 32% of the time, Pallas kernels for 0%

commit v1 on v0

v1 whole, which is shorter than its diff:
```python
import functools

import jax
import jax.numpy as jnp
from jax import lax
from jax.experimental import pallas as pl
from jax.experimental.pallas import tpu as pltpu
from jax.sharding import PartitionSpec as P

D = 768
HEADS = 12
HEAD = 64
PAIR = 2 * HEAD
PAIRS = HEADS // 2
STEP = 10
SEGS = 4

epsilon = 1e-06
score_scale = 0.125
masked_value = -1000000000.0
beta_one = 0.9
beta_two = 0.95
adam_epsilon = 1e-08
decay_matrix = 0.1
rate_matrix = 0.1
rate_gain = 0.3
f32 = jnp.float32
bf16 = jnp.bfloat16
BOTH = ("dp", "fsdp")


def gelu_tanh(values):
    return (
        0.5
        * values
        * (1.0 + jnp.tanh(0.7978845608028654 * (values + 0.044715 * values * values * values)))
    )


def dot_nn(a, b):
    return lax.dot_general(a, b, (((1,), (0,)), ((), ())), preferred_element_type=f32)


def dot_nt(a, b):
    return lax.dot_general(a, b, (((1,), (1,)), ((), ())), preferred_element_type=f32)


def dot_tn(a, b):
    return lax.dot_general(a, b, (((0,), (0,)), ((), ())), preferred_element_type=f32)


def norm_forward(values, gain):
    inverse_rms = lax.rsqrt(jnp.mean(values * values, axis=-1, keepdims=True) + epsilon)
    unit_rows = values * inverse_rms
    return ((unit_rows * gain.astype(f32)).astype(bf16), unit_rows, inverse_rms)


def norm_backward(grad_rows, gain, unit_rows, inverse_rms):
    grad_unit = grad_rows * gain.astype(f32)
    grad_values = inverse_rms * (
        grad_unit - unit_rows * jnp.mean(grad_unit * unit_rows, axis=-1, keepdims=True)
    )
    return (grad_values, jnp.sum(grad_rows * unit_rows, axis=0))


def head_half(block, half):
    lane = lax.broadcasted_iota(jnp.int32, block.shape, 1)
    keep = (lane < HEAD) if half == 0 else (lane >= HEAD)
    return jnp.where(keep, block, jnp.zeros_like(block))


def three_parts(column):
    high = column.astype(bf16).astype(f32)
    rest = column - high
    middle = rest.astype(bf16).astype(f32)
    low = rest - middle
    return high, middle, low


def stat_lanes(base, column, first):
    lane = lax.broadcasted_iota(jnp.int32, base.shape, 1)
    for place, part in enumerate(three_parts(column)):
        base = jnp.where(lane == first + place, -part, base)
    return base


def key_marks(key_ids, stats):
    lane = lax.broadcasted_iota(jnp.int32, (key_ids.shape[0], 128), 1)
    marks = lane == key_ids
    if stats:
        marks = marks | ((lane >= SEGS) & (lane < SEGS + 3))
    return jnp.where(marks, 1.0, 0.0).astype(bf16)


def query_bias(query_ids):
    lane = lax.broadcasted_iota(jnp.int32, (query_ids.shape[0], 128), 1)
    return jnp.where((lane == query_ids) | (lane >= SEGS), 0.0, masked_value)


def softmax_columns(scores):
    top = jnp.max(scores, axis=0, keepdims=True)
    raised = jnp.exp(scores - top)
    return raised, top, jnp.sum(raised, axis=0, keepdims=True)


def finish_forward(halves, tops, sums, o_ref, lse_ref):
    mixed = jnp.concatenate([h / s for h, s in zip(halves, sums)], axis=0)
    o_ref[0] = mixed.T.astype(bf16)
    rows = [t + jnp.log(s) for t, s in zip(tops, sums)]
    pad = jnp.zeros((6, rows[0].shape[1]), f32)
    lse_ref[0, 0] = jnp.concatenate(rows + [pad], axis=0)


def cross_forward_kernel(q_ref, k_ref, v_ref, qid_ref, kid_ref, o_ref, lse_ref):
    marked = jnp.concatenate([k_ref[0], key_marks(kid_ref[0], False)], axis=1)
    bias = query_bias(qid_ref[0]).astype(bf16)
    query = q_ref[0] * jnp.asarray(score_scale, bf16)
    values = v_ref[0].T
    halves, tops, sums = [], [], []
    for half in range(2):
        extended = jnp.concatenate([head_half(query, half), bias], axis=1)
        raised, top, total = softmax_columns(dot_nt(marked, extended))
        halves.append(dot_nn(values[half * HEAD : (half + 1) * HEAD], raised.astype(bf16)))
        tops.append(top)
        sums.append(total)
    finish_forward(halves, tops, sums, o_ref, lse_ref)


def causal_mask(qid_ref, kid_ref):
    length = kid_ref.shape[1]
    key = lax.broadcasted_iota(jnp.int32, (length, length), 0)
    query = lax.broadcasted_iota(jnp.int32, (length, length), 1)
    return (key <= query) & (kid_ref[0] == qid_ref[0])


def self_forward_kernel(q_ref, k_ref, v_ref, qid_ref, kid_ref, o_ref, lse_ref):
    allowed = causal_mask(qid_ref, kid_ref)
    query = q_ref[0] * jnp.asarray(score_scale, bf16)
    key = k_ref[0]
    values = v_ref[0].T
    halves, tops, sums = [], [], []
    for half in range(2):
        scores = jnp.where(allowed, dot_nt(key, head_half(query, half)), masked_value)
        raised, top, total = softmax_columns(scores)
        halves.append(dot_nn(values[half * HEAD : (half + 1) * HEAD], raised.astype(bf16)))
        tops.append(top)
        sums.append(total)
    finish_forward(halves, tops, sums, o_ref, lse_ref)


def backward_pair(q_ref, k_ref, v_ref, o_ref, do_ref, lse_ref, marked, bias, allowed,
                  dq_ref, dk_ref, dv_ref):
    query, grad = q_ref[0], do_ref[0]
    scaled = query * jnp.asarray(score_scale, bf16)
    key_turned = k_ref[0].T
    length = query.shape[0]
    lse_columns = lse_ref[0, 0].T
    product = o_ref[0].astype(f32) * grad.astype(f32)
    ones = key_marks(jnp.full((v_ref.shape[1], 1), -1, jnp.int32), True)
    valued = jnp.concatenate([v_ref[0], ones], axis=1)
    probs, grads, turned = [], [], []
    for half in range(2):
        stats = stat_lanes(bias, lse_columns[:, half : half + 1], SEGS).astype(bf16)
        scores = dot_nt(marked, jnp.concatenate([head_half(scaled, half), stats], axis=1))
        if allowed is not None:
            scores = jnp.where(allowed, scores, masked_value)
        weight = jnp.exp(scores)
        inner = jnp.sum(head_half(product, half), axis=1, keepdims=True)
        delta = stat_lanes(jnp.zeros((length, 128), f32), inner, SEGS).astype(bf16)
        shifted = dot_nt(valued, jnp.concatenate([head_half(grad, half), delta], axis=1))
        grad_scores = (weight * shifted).astype(bf16)
        probs.append(weight.astype(bf16))
        grads.append(grad_scores)
        turned.append(dot_nn(key_turned[half * HEAD : (half + 1) * HEAD], grad_scores))
    dq_ref[0] = (score_scale * jnp.concatenate(turned, axis=0)).T.astype(bf16)
    dv_ref[0] = dot_nn(
        jnp.concatenate(probs, axis=1),
        jnp.concatenate([head_half(grad, 0), head_half(grad, 1)], axis=0),
    ).astype(bf16)
    dk_ref[0] = dot_nn(
        jnp.concatenate(grads, axis=1),
        jnp.concatenate([head_half(scaled, 0), head_half(scaled, 1)], axis=0),
    ).astype(bf16)


def cross_backward_kernel(q_ref, k_ref, v_ref, o_ref, do_ref, lse_ref, qid_ref, kid_ref,
                          dq_ref, dk_ref, dv_ref):
    marked = jnp.concatenate([k_ref[0], key_marks(kid_ref[0], True)], axis=1)
    backward_pair(q_ref, k_ref, v_ref, o_ref, do_ref, lse_ref, marked, query_bias(qid_ref[0]),
                  None, dq_ref, dk_ref, dv_ref)


def self_backward_kernel(q_ref, k_ref, v_ref, o_ref, do_ref, lse_ref, qid_ref, kid_ref,
                         dq_ref, dk_ref, dv_ref):
    length = k_ref.shape[1]
    ones = key_marks(jnp.full((length, 1), -1, jnp.int32), True)
    marked = jnp.concatenate([k_ref[0], ones], axis=1)
    backward_pair(q_ref, k_ref, v_ref, o_ref, do_ref, lse_ref, marked,
                  jnp.zeros((length, 128), f32), causal_mask(qid_ref, kid_ref),
                  dq_ref, dk_ref, dv_ref)


def pair_spec(length, offset):
    return pl.BlockSpec((1, length, PAIR), lambda row, pair: (row, 0, offset + pair))


def row_spec(shape):
    return pl.BlockSpec((1,) + shape, lambda row, pair: (row, 0, 0))


def stat_spec(length):
    return pl.BlockSpec((1, 1, 8, length), lambda row, pair: (row, pair, 0, 0))


def cost(rows, queries, keys, products):
    elements = rows * HEADS * queries * keys
    return pl.CostEstimate(
        flops=2 * elements * 256 * products // 2,
        transcendentals=elements,
        bytes_accessed=rows * (queries + keys) * D * 2 * 3,
    )


def attend_forward(kernel, queries, keys, offsets, query_ids, key_ids, query_shape):
    rows, length = queries.shape[:2]
    count = keys.shape[1]
    return pl.pallas_call(
        kernel,
        grid=(rows, PAIRS),
        in_specs=[
            pair_spec(length, 0),
            pair_spec(count, offsets[0]),
            pair_spec(count, offsets[1]),
            row_spec(query_shape),
            row_spec((count, 1)),
        ],
        out_specs=[pair_spec(length, 0), stat_spec(length)],
        out_shape=[
            jax.ShapeDtypeStruct((rows, length, D), bf16),
            jax.ShapeDtypeStruct((rows, PAIRS, 8, length), f32),
        ],
        cost_estimate=cost(rows, length, count, 2),
    )(queries, keys, keys, query_ids, key_ids)


def attend_backward(kernel, queries, keys, offsets, mixed, grad, lse, query_ids, key_ids,
                    query_shape):
    rows, length = grad.shape[:2]
    count = keys.shape[1]
    return pl.pallas_call(
        kernel,
        grid=(rows, PAIRS),
        in_specs=[
            pair_spec(length, 0),
            pair_spec(count, offsets[0]),
            pair_spec(count, offsets[1]),
            pair_spec(length, 0),
            pair_spec(length, 0),
            stat_spec(length),
            row_spec(query_shape),
            row_spec((count, 1)),
        ],
        out_specs=[pair_spec(length, 0), pair_spec(count, 0), pair_spec(count, 0)],
        out_shape=[
            jax.ShapeDtypeStruct((rows, length, D), bf16),
            jax.ShapeDtypeStruct((rows, count, D), bf16),
            jax.ShapeDtypeStruct((rows, count, D), bf16),
        ],
        cost_estimate=cost(rows, length, count, 5),
    )(queries, keys, keys, mixed, grad, lse, query_ids, key_ids)


def gather_weights(attention, inner, outer):
    turned = lax.all_gather(jnp.swapaxes(attention, 1, 2), BOTH, axis=0, tiled=False)
    heads = lax.axis_size("dp"), lax.axis_size("fsdp")
    turned = turned.reshape(heads + turned.shape[1:])
    full_attention = jnp.transpose(turned, (2, 0, 3, 1, 4)).reshape(8, D, D)
    wide = lax.all_gather(inner, BOTH, axis=0, tiled=False)
    wide = wide.reshape(heads + wide.shape[1:])
    full_inner = jnp.transpose(wide, (2, 1, 3, 0, 4)).reshape(2, D, -1)
    tall = lax.all_gather(outer.T, BOTH, axis=0, tiled=False)
    tall = tall.reshape(heads + tall.shape[1:])
    full_outer = jnp.transpose(tall, (0, 2, 1, 3)).reshape(D, -1)
    return full_attention, full_inner, full_outer


def scatter_grads(attention, inner, outer):
    across, within = lax.axis_size("dp"), lax.axis_size("fsdp")
    blocks = attention.reshape(8, across, D // across, within, D // within)
    blocks = jnp.transpose(blocks, (1, 3, 0, 2, 4))
    blocks = blocks.reshape((across * within,) + blocks.shape[2:])
    own_attention = lax.psum_scatter(blocks, BOTH, scatter_dimension=0, tiled=False)
    blocks = inner.reshape(2, within, D // within, across, inner.shape[2] // across)
    blocks = jnp.transpose(blocks, (3, 1, 0, 2, 4))
    blocks = blocks.reshape((across * within,) + blocks.shape[2:])
    own_inner = lax.psum_scatter(blocks, BOTH, scatter_dimension=0, tiled=False)
    blocks = outer.reshape(across, D // across, within, outer.shape[1] // within)
    blocks = jnp.transpose(blocks, (0, 2, 1, 3))
    blocks = blocks.reshape((across * within,) + blocks.shape[2:])
    own_outer = lax.psum_scatter(blocks, BOTH, scatter_dimension=0, tiled=False)
    return (
        jnp.swapaxes(own_attention, 1, 2).astype(f32),
        own_inner.astype(f32),
        own_outer.T.astype(f32),
    )


def adam_update(weight, mean_old, square_old, gradient, step_rate, decay_rate):
    mean_new = beta_one * mean_old + (1.0 - beta_one) * gradient
    square_new = beta_two * square_old + (1.0 - beta_two) * gradient * gradient
    corrected = (
        mean_new
        / (1.0 - beta_one**STEP)
        / (jnp.sqrt(square_new / (1.0 - beta_two**STEP)) + adam_epsilon)
    )
    master = weight - step_rate * (corrected + decay_rate * weight)
    return (mean_new, square_new, master, master.astype(bf16))


def on_device(
    hidden_in,
    patches,
    token_segments,
    patch_segments,
    cotangent,
    attention_weights,
    attention_means,
    attention_squares,
    inner_weights,
    inner_means,
    inner_squares,
    outer_weights,
    outer_means,
    outer_squares,
    norm_gains,
    gain_means,
    gain_squares,
):
    rows, _, length, _ = hidden_in.shape
    count = patches.shape[2]
    tokens = rows * length
    weights, inner, outer = gather_weights(
        attention_weights.astype(bf16), inner_weights.astype(bf16), outer_weights.astype(bf16)
    )
    gains = lax.all_gather(norm_gains.astype(bf16), "fsdp", axis=1, tiled=True)

    initial = hidden_in.reshape(tokens, D).astype(f32)
    patch_rows = patches.reshape(rows * count, D)
    token_rows = token_segments.reshape(rows, 1, length)
    token_columns = token_segments.reshape(rows, length, 1)
    patch_columns = patch_segments.reshape(rows, count, 1)

    normed_one, unit_one, rms_one = norm_forward(initial, gains[0])
    packed = dot_nt(normed_one, weights[0:3].reshape(3 * D, D)).astype(bf16)
    packed = packed.reshape(rows, length, 3 * D)
    mixture_one, lse_one = attend_forward(
        self_forward_kernel, packed, packed, (PAIRS, 2 * PAIRS), token_rows, token_columns,
        (1, length),
    )
    mixed_one = mixture_one.reshape(tokens, D)
    after_one = initial + dot_nt(mixed_one, weights[3])
    normed_two, unit_two, rms_two = norm_forward(after_one, gains[1])
    cross_query = dot_nt(normed_two, weights[4]).astype(bf16).reshape(rows, length, D)
    cross_pair = dot_nt(patch_rows, weights[5:7].reshape(2 * D, D)).astype(bf16)
    cross_pair = cross_pair.reshape(rows, count, 2 * D)
    mixture_two, lse_two = attend_forward(
        cross_forward_kernel, cross_query, cross_pair, (0, PAIRS), token_columns, patch_columns,
        (length, 1),
    )
    mixed_two = mixture_two.reshape(tokens, D)
    after_two = after_one + dot_nt(mixed_two, weights[7])
    normed_three, unit_three, rms_three = norm_forward(after_two, gains[2])
    gate = dot_nn(normed_three, inner[0])
    up = dot_nn(normed_three, inner[1])
    units = (gelu_tanh(gate) * up).astype(bf16)
    hidden_out = (after_two + dot_nt(units, outer)).astype(bf16)

    grad_low = cotangent.reshape(tokens, D)
    grad_final = grad_low.astype(f32)
    grad_outer = dot_tn(grad_low, units).astype(bf16)
    grad_units = dot_nn(grad_low, outer)
    activation, gelu_back = jax.vjp(gelu_tanh, gate)
    grad_gate = gelu_back(grad_units * up)[0].astype(bf16)
    grad_up = (grad_units * activation).astype(bf16)
    grad_inner = jnp.stack(
        [dot_tn(normed_three, grad_gate).astype(bf16), dot_tn(normed_three, grad_up).astype(bf16)]
    )
    grad_normed = dot_nt(grad_gate, inner[0]) + dot_nt(grad_up, inner[1])
    grad_from_three, gain_three = norm_backward(grad_normed, gains[2], unit_three, rms_three)
    grad_two = grad_final + grad_from_three
    branch_two = grad_two.astype(bf16)
    grad_mixture_two = dot_nn(branch_two, weights[7]).astype(bf16).reshape(rows, length, D)
    grad_cq, grad_ck, grad_cv = attend_backward(
        cross_backward_kernel, cross_query, cross_pair, (0, PAIRS), mixture_two,
        grad_mixture_two, lse_two, token_columns, patch_columns, (length, 1),
    )
    grad_cq = grad_cq.reshape(tokens, D)
    grad_ck = grad_ck.reshape(rows * count, D)
    grad_cv = grad_cv.reshape(rows * count, D)
    patch_grad = dot_nn(grad_ck, weights[5]) + dot_nn(grad_cv, weights[6])
    grad_from_two, gain_two = norm_backward(
        dot_nn(grad_cq, weights[4]), gains[1], unit_two, rms_two
    )
    grad_one = grad_two + grad_from_two
    branch_one = grad_one.astype(bf16)
    grad_mixture_one = dot_nn(branch_one, weights[3]).astype(bf16).reshape(rows, length, D)
    grad_q, grad_k, grad_v = attend_backward(
        self_backward_kernel, packed, packed, (PAIRS, 2 * PAIRS), mixture_one,
        grad_mixture_one, lse_one, token_rows, token_columns, (1, length),
    )
    grad_q = grad_q.reshape(tokens, D)
    grad_k = grad_k.reshape(tokens, D)
    grad_v = grad_v.reshape(tokens, D)
    grad_normed_one = (
        dot_nn(grad_q, weights[0]) + dot_nn(grad_k, weights[1]) + dot_nn(grad_v, weights[2])
    )
    grad_from_one, gain_one = norm_backward(grad_normed_one, gains[0], unit_one, rms_one)
    hidden_grad = grad_one + grad_from_one
    grad_attention = jnp.stack(
        [
            dot_tn(grad_q, normed_one).astype(bf16),
            dot_tn(grad_k, normed_one).astype(bf16),
            dot_tn(grad_v, normed_one).astype(bf16),
            dot_tn(branch_one, mixed_one).astype(bf16),
            dot_tn(grad_cq, normed_two).astype(bf16),
            dot_tn(grad_ck, patch_rows).astype(bf16),
            dot_tn(grad_cv, patch_rows).astype(bf16),
            dot_tn(branch_two, mixed_two).astype(bf16),
        ]
    )
    own_attention, own_inner, own_outer = scatter_grads(grad_attention, grad_inner, grad_outer)
    gain_totals = lax.psum(jnp.stack([gain_one, gain_two, gain_three]), BOTH)
    width = norm_gains.shape[1]
    own_gains = lax.dynamic_slice_in_dim(
        gain_totals, lax.axis_index("fsdp") * width, width, axis=1
    )

    attention_new = adam_update(
        attention_weights, attention_means, attention_squares, own_attention,
        rate_matrix, decay_matrix,
    )
    inner_new = adam_update(
        inner_weights, inner_means, inner_squares, own_inner, rate_matrix, decay_matrix
    )
    outer_new = adam_update(
        outer_weights, outer_means, outer_squares, own_outer, rate_matrix, decay_matrix
    )
    gain_new = adam_update(norm_gains, gain_means, gain_squares, own_gains, rate_gain, 0.0)
    return (
        hidden_out.reshape(hidden_in.shape),
        hidden_grad.reshape(hidden_in.shape),
        patch_grad.reshape(patches.shape),
        *attention_new,
        *inner_new,
        *outer_new,
        *gain_new,
    )


def solution(mesh):
    rows = P(None, BOTH, None, None)
    ids = P(None, BOTH, None)
    matrix = P(None, "fsdp", "dp")
    down = P("fsdp", "dp")
    gain = P(None, "fsdp")
    return jax.shard_map(
        on_device,
        mesh=mesh,
        in_specs=(rows, rows, ids, ids, rows) + (matrix,) * 6 + (down,) * 3 + (gain,) * 3,
        out_specs=(rows, rows, rows) + (matrix,) * 8 + (down,) * 4 + (gain,) * 4,
        check_vma=False,
    )
```

time: 1280 us -> 808 us (0.63)
  waiting for transfers between devices: 686 us -> 286 us
  matrix products: 296 us -> 127 us
  Pallas kernels: 0 us -> 106 us
  other arithmetic: 75.5 us -> 18.1 us
  local copies, waits for them, and re-layouts: 161 us -> 198 us
    reduce_scatter x4 -> x3, waiting for transfers between devices: 446 us -> 86.7 us  [the longest x1 86.7 us: scatter_grads(): lax.psum_scatter(blocks, BOTH, scatter_dimension=0, tiled=False)]
    dot_general x62 -> x30, matrix products: 259 us -> 127 us  [the longest x11 48.2 us: dot_tn(): lax.dot_general(a, b, (((0,), (0,)), ((), ())), preferred_element_type=f32)]
    pallas_call x0 -> x4, Pallas kernels: none -> 106 us  [the longest x2 57.9 us: attend_backward(): pl.pallas_call(kernel, grid=(rows, PAIRS), in_specs=[pair_spec(length, 0)...]
    reshape x0 -> x8, local copies, waits for them, and re-layouts: none -> 50.6 us  [the longest x1 17.7 us: gather_weights(): turned = turned.reshape(heads + turned.shape[1:])]
    unnamed x293 -> x149, local copies, waits for them, and re-layouts: 80.4 us -> 34.1 us
    unnamed x14 -> x6, waiting for transfers between devices: 39 us -> 0.1 us
    sub x4 -> x0, matrix products: 37.1 us -> none  [softmax_rows(): raised = jnp.exp(scores - row_maximum)]
    transpose x0 -> x3, local copies, waits for them, and re-layouts: none -> 32.5 us  [the longest x1 24 us: scatter_grads(): blocks = jnp.transpose(blocks, (1, 3, 0, 2, 4))]
  transfers between devices with their start and end apart: 11 -> 6, of which waited for: 9 -> 4; matrix products, arithmetic and copies ran while one was open for 32% -> 27% of each run, Pallas kernels for 0% -> 7%
where the time goes in v1:
time: 808 us; the launch traced here: 796 us
  waiting for transfers between devices  286 us (35%)
  local copies, waits for them, and re-layouts  198 us (25%)
  matrix products  127 us (16%)
  Pallas kernels  106 us (13%)
  blocking collectives  45.6 us (6%)
  other arithmetic  18.1 us (2%)
  between operations  15.2 us (2%)
    reduce_scatter x1, waiting for transfers between devices, scatter_grads(): lax.psum_scatter(blocks, BOTH, scatter_dimension=0, tiled=False)  86.7 us
    all_gather x1, waiting for transfers between devices, gather_weights(): lax.all_gather(jnp.swapaxes(attention, 1, 2), BOTH, axis=0, tiled=False)  84.5 us
    all_gather x1, waiting for transfers between devices, gather_weights(): wide = lax.all_gather(inner, BOTH, axis=0, tiled=False)  64.4 us
    pallas_call x2, Pallas kernels, attend_backward(): pl.pallas_call(kernel, grid=(rows, PAIRS), in_specs=[pair_spec(length, 0)...  57.9 us
    all_gather x1, waiting for transfers between devices, gather_weights(): tall = lax.all_gather(outer.T, BOTH, axis=0, tiled=False)  49.9 us
    dot_general x11, matrix products, dot_tn(): lax.dot_general(a, b, (((0,), (0,)), ((), ())), preferred_element_type=f32)  48.2 us
    pallas_call x2, Pallas kernels, attend_forward(): pl.pallas_call(kernel, grid=(rows, PAIRS), in_specs=[pair_spec(length, 0)...  47.9 us
    dot_general x11, matrix products, dot_nn(): lax.dot_general(a, b, (((1,), (0,)), ((), ())), preferred_element_type=f32)  42.1 us
  transfers between devices with their start and end apart: 6, of which 4 were waited for; matrix products, arithmetic and copies ran while one was open for 27% of the time, Pallas kernels for 7%

profile of v1, /device:TPU:0, one launch (start us, length us, event | category | flops | bytes accessed | tf_op | source)
XLA Modules:
  0.0 796.3 jit_solution(12030855078380946646)
XLA Ops:
  11.8 6.3 all-gather.3
  23.4 49.9 %all-gather.12.cloned.1.call-done = bf16[3072,512]{1,0:T(8,128)(2,1)} async-done(((bf16[96,512]{1,0:T(8,128)(2,1)}), bf16[3072,512]{1,0:T(8,128)(2,1)}) %all-gather.12.cloned.1.call-update) | async-done | bytes 3145744 | tf_op jit(solution)/shard_map/all_gather | solution.py:281
  73.3 4.3 copy.88
  80.3 64.4 %all-gather.10.cloned.1.call-done = bf16[64,192,256]{2,1,0:T(8,128)(2,1)} async-done(((bf16[2,192,256]{2,1,0:T(8,128)(2,1)}), bf16[64,192,256]{2,1,0:T(8,128)(2,1)}) %all-gather.10.cloned.1.call-update) | async-done | bytes 6291472 | tf_op jit(solution)/shard_map/all_gather | solution.py:278
  144.7 6.6 copy.106
  157.3 84.5 %all-gather.8.cloned.1.call-done = bf16[256,96,192]{2,1,0:T(8,128)(2,1)} async-done(((bf16[8,96,192]{2,1,0:T(8,128)(2,1)}), bf16[256,96,192]{2,1,0:T(8,128)(2,1)}) %all-gather.8.cloned.1.call-update) | async-done | bytes 9437200 | tf_op jit(solution)/shard_map/all_gather | solution.py:274
  241.9 17.7 %copy.81 = bf16[8,4,8,96,192]{3,0,4,1,2:T(8,128)(2,1)} copy(bf16[8,4,8,96,192]{4,3,2,1,0:T(8,128)(2,1)} %bitcast.240) | data formatting | bytes 18874368 | tf_op jit(solution)/shard_map/reshape | solution.py:276
  261.9 5.4 slice.81
  268.2 4.7 fusion.46
  273.4 4.5 reshape.292
  277.9 5.3 copy.82
  283.2 8.1 %reshape.286 = bf16[2304,768]{0,1:T(8,128)(2,1)} reshape(bf16[3,8,96,4,192]{2,1,0,4,3:T(8,128)(2,1)} %copy.82) | data formatting | bytes 7077888 | tf_op jit(solution)/shard_map/reshape | solution.py:354
  297.7 5.4 convolution_convert_fusion.1
  303.2 12.0 %shard_map.312 = (bf16[2,256,768]{2,1,0:T(8,128)(2,1)}, f32[2,6,8,256]{3,2,1,0:T(8,128)}) custom-call(bf16[2,256,2304]{2,1,0:T(8,128)(2,1)} %bitcast.227, bf16[2,256,2304]{2,1,0:T(8,128)(2,1)} %bitcast.228, bf16[2,256,2304]{2,1,0:T(8,128)(2,1)} %bitcast.229, s32[2,1,256]{2,1,0:T(1,128)} %qid_ref.3, s32[2,256,1]{2,1,0:T(8,128)} %reshape.330.kid_ref.qid_ref), custom_call_target="tpu_custom_call" | custom-call | flops 805306368 | bytes 4718592 | tf_op jit(solution)/shard_map/pallas_call | solution.py:227
  317.7 16.1 %convolution_convert_fusion = bf16[4096,1536]{1,0:T(8,128)(2,1)} fusion(bf16[4096,768]{1,0:T(8,128)(2,1)} %bitcast.278, bf16[1536,768]{0,1:T(8,128)(2,1)S(1)} %copy-done.31), kind=kOutput, calls=%fused_computation | convolution fusion | flops 9669967872 | bytes 21233664 | tf_op jit(solution)/shard_map/dot_general | solution.py:45
  335.6 35.9 %shard_map.313 = (bf16[2,256,768]{2,1,0:T(8,128)(2,1)}, f32[2,6,8,256]{3,2,1,0:T(8,128)}) custom-call(bf16[2,256,768]{2,1,0:T(8,128)(2,1)} %bitcast.264, bf16[2,2048,1536]{2,1,0:T(8,128)(2,1)} %bitcast.233, bf16[2,2048,1536]{2,1,0:T(8,128)(2,1)} %bitcast.234, s32[2,256,1]{2,1,0:T(8,128)} %reshape.330.kid_ref.qid_ref, s32[2,2048,1]{2,1,0:T(8,128)} %reshape.331.kid_ref), custom_call_target="tpu_custom_call" | custom-call | flops 6442450944 | bytes 21233664 | tf_op jit(solution)/shard_map/pallas_call | solution.py:227
  378.6 7.2 multiply_convert_fusion
  387.1 3.5 fusion.6
  390.7 4.7 copy.94
  395.4 6.2 reshape.313
  401.5 4.4 copy.95
  406.2 3.4 convolution_convert_fusion.3
  414.8 4.0 copy.93
  426.9 42.0 %shard_map.314 = (bf16[2,256,768]{2,1,0:T(8,128)(2,1)}, bf16[2,2048,768]{2,1,0:T(8,128)(2,1)}, bf16[2,2048,768]{2,1,0:T(8,128)(2,1)}) custom-call(bf16[2,256,768]{2,1,0:T(8,128)(2,1)} %bitcast.265, bf16[2,2048,1536]{2,1,0:T(8,128)(2,1)} %bitcast.235, bf16[2,2048,1536]{2,1,0:T(8,128)(2,1)} %bitcast.236, bf16[2,256,768]{2,1,0:T(8,128)(2,1)} %get-tuple-element.30.o_ref, ...), custom_call_target="tpu_custom_call" | custom-call | flops 16106127360 | bytes 21233664 | tf_op jit(solution)/shard_map/pallas_call | solution.py:250
  474.5 16.0 %shard_map.315 = (bf16[2,256,768]{2,1,0:T(8,128)(2,1)}, bf16[2,256,768]{2,1,0:T(8,128)(2,1)}, bf16[2,256,768]{2,1,0:T(8,128)(2,1)}) custom-call(bf16[2,256,2304]{2,1,0:T(8,128)(2,1)} %bitcast.230, bf16[2,256,2304]{2,1,0:T(8,128)(2,1)} %bitcast.231, bf16[2,256,2304]{2,1,0:T(8,128)(2,1)} %bitcast.232, bf16[2,256,768]{2,1,0:T(8,128)(2,1)} %get-tuple-element.29.o_ref, ...), custom_call_target="tpu_custom_call" | custom-call | flops 2013265920 | bytes 4718592 | tf_op jit(solution)/shard_map/pallas_call | solution.py:250
  490.5 3.2 convolution_convert_fusion.11
  493.7 4.4 stack.49
  501.0 4.4 stack.51
  505.4 3.2 convolution_convert_fusion.12
  508.6 4.8 stack.48
  513.4 3.2 convolution_convert_fusion.10
  516.6 4.4 stack.50
  524.0 3.5 stack.55
  527.5 3.6 convolution_convert_fusion.8
  531.2 4.4 stack.52
  535.6 10.1 %convolution_convert_fusion.7 = bf16[768,768]{1,0:T(8,128)(2,1)} fusion(bf16[4096,768]{1,0:T(8,128)(2,1)} %bitcast.290, bf16[4096,768]{1,0:T(8,128)(2,1)} %bitcast.279), kind=kOutput, calls=%fused_computation.51 | convolution fusion | flops 4832428032 | bytes 13762560 | tf_op jit(solution)/shard_map/dot_general | solution.py:49
  545.7 4.4 stack.53
  550.1 10.1 %convolution_convert_fusion.6 = bf16[768,768]{1,0:T(8,128)(2,1)} fusion(bf16[4096,768]{1,0:T(8,128)(2,1)} %bitcast.286, bf16[4096,768]{1,0:T(8,128)(2,1)} %bitcast.280), kind=kOutput, calls=%fused_computation.50 | convolution fusion | flops 4832428032 | bytes 13762560 | tf_op jit(solution)/shard_map/dot_general | solution.py:49
  560.2 4.5 stack.54
  564.7 3.2 constant_dynamic-update-slice_fusion.7
  580.2 24.0 %copy.92 = bf16[8,4,8,96,192]{3,4,2,1,0:T(8,128)(2,1)} copy(bf16[8,4,8,96,192]{4,1,3,0,2:T(4,128)(2,1)} %bitcast.34) | data formatting | bytes 18874368 | tf_op jit(solution)/shard_map/transpose | solution.py:290
  607.8 3.9 squeeze.49
  613.8 3.9 squeeze.47
  626.7 39.3 %psum.7 = f32[3,768]{1,0:T(4,128)S(1)} all-reduce(f32[3,768]{1,0:T(4,128)S(1)} %pad_maximum_fusion), channel_id=1, replica_groups=mesh['dp'=8,'fsdp'=4] {'dp','fsdp'}, use_global_device_ids=true, to_apply=%region_12.0 | all-reduce | flops 2304 | bytes 18432 | tf_op jit(solution)/shard_map/psum | solution.py:432
  670.4 5.0 add_convert_fusion
  675.4 8.3 %fusion.53 = f32[4096,768]{1,0:T(8,128)} fusion(bf16[4096,768]{1,0:T(8,128)(2,1)S(1)} %bitcast.293, bf16[768,768]{0,1:T(8,128)(2,1)S(1)} %copy-done.36), kind=kOutput, calls=%fused_computation.124 | convolution fusion | flops 4831838208 | bytes 20054016 | tf_op jit(solution)/shard_map/dot_general | solution.py:41
  683.8 11.3 %convolution_add_fusion = f32[4096,768]{1,0:T(8,128)} fusion(f32[4096,768]{1,0:T(8,128)} %fusion.53, bf16[4096,768]{1,0:T(8,128)(2,1)S(1)} %bitcast.289, bf16[768,768]{0,1:T(8,128)(2,1)S(1)} %copy-done.35), kind=kOutput, calls=%fused_computation.7 | convolution fusion | flops 4834983936 | bytes 32636928 | tf_op jit(solution)/shard_map/dot_general | solution.py:41
  699.4 86.7 %reduce-scatter.4.cloned.1.call-done = bf16[1,8,96,192]{2,3,1,0:T(8,128)(2,1)} async-done(((bf16[32,8,96,192]{2,3,1,0:T(8,128)(2,1)}), bf16[1,8,96,192]{2,3,1,0:T(8,128)(2,1)}) %reduce-scatter.4.cloned.1.call-update) | async-done | bytes 294928 | tf_op jit(solution)/shard_map/reduce_scatter | solution.py:292
  (220 shorter events, 104.6 us)
Async XLA Ops:
  7.2 3.6 copy-start.29
  7.2 4.6 copy-start.52
  7.2 11.0 %copy-start.51 = (s32[2,1,256]{2,1,0:T(1,128)S(1)}, s32[2,1,256]{2,1,0:T(1,128)}, u32[]{:S(2)}) copy-start(s32[2,1,256]{2,1,0:T(1,128)} %qid_ref.3) | copy-start | bytes 6148
  7.2 11.0 %copy-start.54 = (s32[2,1,2048]{2,1,0:T(1,128)S(1)}, s32[2,1,2048]{2,1,0:T(1,128)}, u32[]{:S(2)}) copy-start(s32[2,1,2048]{2,1,0:T(1,128)} %param.20) | copy-start | bytes 49156
  7.2 66.1 %all-gather.12.cloned.1.call-start = ((), (), s32[]{:S(2)}) async-start(), calls=%async_computation.8 | async-start | bytes 3244032 | tf_op jit(solution)/shard_map/all_gather | solution.py:281
  8.9 135.7 %all-gather.10.cloned.1.call-start = ((), (), s32[]{:S(2)}) async-start(), calls=%async_computation.7 | async-start | bytes 6488064 | tf_op jit(solution)/shard_map/all_gather | solution.py:278
  10.7 231.1 %all-gather.8.cloned.1.call-start = ((), (), s32[]{:S(2)}) async-start(), calls=%async_computation.6 | async-start | bytes 12976128 | tf_op jit(solution)/shard_map/all_gather | solution.py:274
  11.7 9.7 %copy-start.3 = (bf16[2,1,256,768]{3,2,1,0:T(8,128)(2,1)S(1)}, bf16[2,1,256,768]{3,2,1,0:T(8,128)(2,1)}, u32[]{:S(2)}) copy-start(bf16[2,1,256,768]{3,2,1,0:T(8,128)(2,1)} %param.17) | copy-start | bytes 2359300
  11.7 683.3 %reduce-scatter.8.cloned.1.call-start = ((), (), s32[]{:S(2)}) async-start(), calls=%async_computation.5 | async-start | bytes 3244032 | tf_op jit(solution)/shard_map/reduce_scatter | solution.py:300
  259.6 8.6 %copy-start = (bf16[8,4,8,96,192]{3,0,4,1,2:T(8,128)(2,1)S(1)}, bf16[8,4,8,96,192]{3,0,4,1,2:T(8,128)(2,1)}, u32[]{:S(2)}) copy-start(bf16[8,4,8,96,192]{3,0,4,1,2:T(8,128)(2,1)} %copy.81) | copy-start | bytes 28311556
  283.2 8.1 %copy-start.11 = (bf16[1,8,96,4,192]{2,1,4,3,0:T(8,128)(2,1)S(1)}, bf16[1,8,96,4,192]{2,1,4,3,0:T(8,128)(2,1)}, u32[]{:S(2)}) copy-start(bf16[1,8,96,4,192]{2,1,4,3,0:T(8,128)(2,1)} %get-tuple-element.145) | copy-start | bytes 3538948
  303.2 12.0 %copy-start.4 = (bf16[2,1,256,768]{3,2,1,0:T(8,128)(2,1)S(1)}, bf16[2,1,256,768]{3,2,1,0:T(8,128)(2,1)}, u32[]{:S(2)}) copy-start(bf16[2,1,256,768]{3,2,1,0:T(8,128)(2,1)} %param.17) | copy-start | bytes 2359300
  315.2 2.6 copy-start.31
  317.7 53.8 %copy-start.18 = (f32[512,768]{1,0:T(8,128)}, f32[512,768]{1,0:T(8,128)S(1)}, u32[]{:S(2)}) copy-start(f32[512,768]{1,0:T(8,128)S(1)} %get-tuple-element.156) | copy-start | bytes 4718596
  317.7 16.1 %copy-start.34 = (bf16[768,768]{0,1:T(8,128)(2,1)S(1)}, bf16[768,768]{0,1:T(8,128)(2,1)}, u32[]{:S(2)}) copy-start(bf16[768,768]{0,1:T(8,128)(2,1)} %squeeze.42) | copy-start | bytes 3538948
  371.5 2.8 copy-start.25
  374.0 49.5 %copy-start.1 = (f32[512,768]{1,0:T(8,128)}, f32[512,768]{1,0:T(8,128)S(1)}, u32[]{:S(2)}) copy-start(f32[512,768]{1,0:T(8,128)S(1)} %get-tuple-element.158) | copy-start | bytes 4718596
  374.3 2.2 copy-start.27
  406.0 291.1 %reduce-scatter.6.cloned.1.call-start = ((), (), s32[]{:S(2)}) async-start(), calls=%async_computation.4 | async-start | bytes 6488064 | tf_op jit(solution)/shard_map/reduce_scatter | solution.py:296
  414.7 4.1 copy-start.28
  414.7 4.0 copy-start.61
  418.8 2.6 copy-start.59
  421.4 2.2 copy-start.41
  426.7 359.4 %reduce-scatter.4.cloned.1.call-start = ((), (), s32[]{:S(2)}) async-start(), calls=%async_computation.3 | async-start | bytes 12976128 | tf_op jit(solution)/shard_map/reduce_scatter | solution.py:292
  426.9 42.0 %copy-start.19 = (f32[512,768]{1,0:T(8,128)S(1)}, f32[512,768]{1,0:T(8,128)}, u32[]{:S(2)}) copy-start(f32[512,768]{1,0:T(8,128)} %copy-done.18) | copy-start | bytes 4718596
  468.9 2.6 copy-start.20
  564.7 3.2 copy-start.13
  607.8 3.9 copy-start.7
  613.8 3.9 copy-start.6
  620.1 2.5 copy-start.37
  620.1 2.5 copy-start.58
  624.4 41.6 %copy-start.53 = (f32[3,192]{1,0:T(4,128)S(1)}, f32[3,192]{1,0:T(4,128)}, u32[]{:S(2)}) copy-start(f32[3,192]{1,0:T(4,128)} %param.31) | copy-start | bytes 6916
  624.4 41.6 %copy-start.56 = (f32[3,192]{1,0:T(4,128)S(1)}, f32[3,192]{1,0:T(4,128)}, u32[]{:S(2)}) copy-start(f32[3,192]{1,0:T(4,128)} %param.33) | copy-start | bytes 6916
  624.4 41.6 %copy-start.57 = (f32[3,192]{1,0:T(4,128)S(1)}, f32[3,192]{1,0:T(4,128)}, u32[]{:S(2)}) copy-start(f32[3,192]{1,0:T(4,128)} %param.32) | copy-start | bytes 6916
  666.7 3.2 copy-start.2
  666.7 3.7 copy-start.24
  666.7 8.7 %slice-start.2 = ((s8[6291456]{0:T(1024)(128)(4,1)}), s8[4194304]{0:T(1024)(128)(4,1)S(1)}, s32[]{:S(2)}) async-start(s8[6291456]{0:T(1024)(128)(4,1)} %bitcast.291), calls=%async_computation.11 | async-start | bytes 8388608
  670.4 5.0 copy-start.36
  670.4 5.0 slice-start.3
  670.4 13.3 %slice-start = ((s8[6291456]{0:T(1024)(128)(4,1)}), s8[4194304]{0:T(1024)(128)(4,1)S(1)}, s32[]{:S(2)}) async-start(s8[6291456]{0:T(1024)(128)(4,1)} %bitcast.287), calls=%async_computation.9 | async-start | bytes 8388608
  675.4 8.3 %copy-start.35 = (bf16[768,768]{0,1:T(8,128)(2,1)S(1)}, bf16[768,768]{0,1:T(8,128)(2,1)}, u32[]{:S(2)}) copy-start(bf16[768,768]{0,1:T(8,128)(2,1)} %squeeze.50) | copy-start | bytes 3538948
  675.4 8.3 %slice-start.1 = ((s8[6291456]{0:T(1024)(128)(4,1)}), s8[2097152]{0:T(1024)(128)(4,1)S(1)}, s32[]{:S(2)}) async-start(s8[6291456]{0:T(1024)(128)(4,1)} %bitcast.287), calls=%async_computation.10 | async-start | bytes 4194304
  683.7 11.4 %copy-start.39 = (f32[512,96]{0,1:T(8,128)S(1)}, f32[512,96]{0,1:T(8,128)}, u32[]{:S(2)}) copy-start(f32[512,96]{0,1:T(8,128)} %param.28) | copy-start | bytes 589828
  683.8 11.4 %copy-start.47 = (f32[512,96]{0,1:T(8,128)S(1)}, f32[512,96]{0,1:T(8,128)}, u32[]{:S(2)}) copy-start(f32[512,96]{0,1:T(8,128)} %param.30) | copy-start | bytes 589828
  683.8 11.4 %copy-start.48 = (f32[512,96]{0,1:T(8,128)S(1)}, f32[512,96]{0,1:T(8,128)}, u32[]{:S(2)}) copy-start(f32[512,96]{0,1:T(8,128)} %param.29) | copy-start | bytes 589828
  697.0 89.1 %copy-start.30 = (f32[8,192,96]{2,1,0:T(8,128)S(1)}, f32[8,192,96]{2,1,0:T(8,128)}, u32[]{:S(2)}) copy-start(f32[8,192,96]{2,1,0:T(8,128)} %param.22) | copy-start | bytes 1769476
  697.0 89.1 %copy-start.42 = (f32[8,192,96]{2,1,0:T(8,128)S(1)}, f32[8,192,96]{2,1,0:T(8,128)}, u32[]{:S(2)}) copy-start(f32[8,192,96]{2,1,0:T(8,128)} %param.24) | copy-start | bytes 1769476
  697.0 89.1 %copy-start.43 = (f32[8,192,96]{2,1,0:T(8,128)S(1)}, f32[8,192,96]{2,1,0:T(8,128)}, u32[]{:S(2)}) copy-start(f32[8,192,96]{2,1,0:T(8,128)} %param.23) | copy-start | bytes 1769476
  (25 other events, 41.6 us)
Sparse Core Ops, SparseCore 0:
  11.5 61.7 all-gather.11
  76.8 67.8 all-gather.9
  148.1 93.6 all-gather.7
  406.1 100.6 reduce-scatter.7
  512.3 113.9 reduce-scatter.5
  632.2 153.8 reduce-scatter.3
